TPU v7x, 32 devices: a whole 2x2x4 slice. The times are simulated.
32 devices in a mesh: client: 8 (over z, x), head: 4 (over y, core).
Axes of the slice: x: 2, y: 2, z: 4, core: 2. Of those that a mesh axis runs over, the one named last changes fastest.
Arguments:
- pre: bfloat16 [10240, 4096], P('client'), may hold values from -40 to 40
- delta: float32 [10240, 4096], P('client', 'head'), may hold values from -300 to 300
- head_weight: bfloat16 [4096, 4096], P(None, 'head'), may hold values from -0.09375 to 0.09375
- client_ids: int32 [128], P('client'), may hold values from 0 to 127, as said below
Outputs:
- head_grad: float32 [4096, 4096], P('client', 'head')
- bias_grad: float32 [4096], P('head')
- embed_grad: float32 [128, 4096], P('client', 'head')
- span_grad: float32 [80, 4096], P(None, 'head')
Inputs may be any that keep to these rules, and one draw needn't show every extreme that they name: `client_ids`: each of the 128 clients appears exactly once.
All inputs are finite; a program needn't handle non-finite values.
Results may differ from a plain program's by a relative error of at most 0.024.
Values may be sent and summed in bfloat16 or wider, within the bound.
A program may use at most 128 MiB of HBM per device.

v0:
```python
import jax
import jax.numpy as jnp
from jax import lax
from jax.sharding import PartitionSpec as P

EPSILON = 1e-06


def silu_slope(values):
    sigma = jax.nn.sigmoid(values)
    return sigma * (1.0 + values * (1.0 - sigma))


def clip_factor(total, number):
    return jnp.minimum(1.0, 1.0 / jnp.sqrt(total / number + EPSILON))


def per_device(pre, delta, head_weight, client_ids):
    rows_here, hidden_width = pre.shape
    emit_here = delta.shape[1]
    clients_here = client_ids.shape[0]
    span_count = rows_here // clients_here
    head_devices = lax.axis_size("head")
    client_devices = lax.axis_size("client")
    hidden = jax.nn.silu(pre.astype(jnp.float32)).astype(jnp.bfloat16)
    delta_low = delta.astype(jnp.bfloat16)
    head_raw = lax.psum_scatter(
        lax.dot_general(
            hidden, delta_low, (((0,), (0,)), ((), ())), preferred_element_type=jnp.float32
        ).astype(jnp.bfloat16),
        "client",
        scatter_dimension=0,
        tiled=True,
    ).astype(jnp.float32)
    head_square = jnp.sum(head_raw * head_raw)
    head_square = lax.psum(head_square, ("client", "head"))
    bias_local = jnp.sum(delta, axis=0)
    partial_sum = lax.dot_general(
        delta_low, head_weight, (((1,), (1,)), ((), ())), preferred_element_type=jnp.float32
    )
    rounded = lax.optimization_barrier(partial_sum.astype(jnp.bfloat16))
    block_grad = rounded.astype(jnp.float32) * silu_slope(pre.astype(jnp.float32))
    grouped = block_grad.reshape(clients_here, span_count, hidden_width)
    client_whole = jnp.sum(grouped, axis=1)
    span_whole = jnp.sum(grouped, axis=0)
    client_part, span_part = (
        lax.psum_scatter(
            client_whole.astype(jnp.bfloat16), "head", scatter_dimension=1, tiled=True
        ).astype(jnp.float32),
        lax.psum_scatter(
            span_whole.astype(jnp.bfloat16), "head", scatter_dimension=1, tiled=True
        ).astype(jnp.float32),
    )
    span_raw, bias_raw = (
        lax.psum(span_part.astype(jnp.bfloat16), "client").astype(jnp.float32),
        lax.psum(bias_local.astype(jnp.bfloat16), "client").astype(jnp.float32),
    )
    targets = lax.iota(jnp.int32, lax.axis_size("client") * clients_here)
    selector = (targets[:, None] == client_ids[None, :]).astype(jnp.float32)
    embed_raw = lax.psum_scatter(
        jnp.dot(
            selector,
            client_part,
            precision=lax.Precision.HIGHEST,
            preferred_element_type=jnp.float32,
        ).astype(jnp.bfloat16),
        "client",
        scatter_dimension=0,
        tiled=True,
    ).astype(jnp.float32)
    leading = (lax.axis_index("client") == 0).astype(jnp.float32)
    small_square = leading * (jnp.sum(span_raw * span_raw) + jnp.sum(bias_raw * bias_raw))
    embed_square = jnp.sum(embed_raw * embed_raw)
    embed_total, small_total = lax.psum((embed_square, small_square), ("client", "head"))
    emit_total = emit_here * head_devices
    clients_total = clients_here * client_devices
    head_factor = clip_factor(head_square, hidden_width * emit_total)
    embed_factor = clip_factor(embed_total, clients_total * hidden_width)
    rest_factor = clip_factor(small_total, span_count * hidden_width + emit_total)
    return (
        head_factor * head_raw,
        rest_factor * bias_raw,
        embed_factor * embed_raw,
        rest_factor * span_raw,
    )


def solution(mesh):
    placed = (P("client", None), P("client", "head"), P(None, "head"), P("client"))
    return jax.shard_map(
        per_device,
        mesh=mesh,
        in_specs=placed,
        out_specs=(P("client", "head"), P("head"), P("client", "head"), P(None, "head")),
        check_vma=False,
    )
```

profile of v0, /device:TPU:0, one launch (start us, length us, event | category | flops | bytes accessed | tf_op | source)
XLA Modules:
  0.0 433.6 jit_solution(12990887152646815512)
XLA Ops:
  7.2 0.0 reduce-scatter.9.cloned.1.call-start
  7.2 0.0 copy-start
  7.2 17.6 %convolution_convert_fusion = bf16[1280,4096]{1,0:T(8,128)(2,1)} fusion(bf16[4096,1024]{1,0:T(8,128)(2,1)} %param.6, f32[1280,1024]{1,0:T(8,128)} %param.5), kind=kOutput, calls=%fused_computation.10 | convolution fusion | flops 10743971840 | bytes 24117248 | tf_op jit(solution)/shard_map/dot_general | solution.py:38
  24.8 9.6 %fusion.6 = f32[1280,4096]{1,0:T(8,128)S(1)} fusion(bf16[1280,4096]{1,0:T(8,128)(2,1)S(1)} %copy-done, bf16[1280,4096]{1,0:T(8,128)(2,1)} %convolution_convert_fusion), kind=kLoop, calls=%fused_computation.9 | loop fusion | flops 52428800 | bytes 41943040 | tf_op jit(solution)/shard_map/mul | solution.py:42
  34.4 5.2 %fusion.20 = (bf16[16,4096]{1,0:T(8,128)(2,1)}, bf16[80,4096]{1,0:T(8,128)(2,1)}) fusion(f32[16,80,4096]{2,1,0:T(8,128)S(1)} %bitcast.3), kind=kLoop, calls=%fused_computation.31 | loop fusion | flops 10092544 | bytes 21757952 | tf_op jit(solution)/shard_map/reduce_sum | solution.py:44
  39.5 0.0 reduce-scatter.9.cloned.1.call-update
  39.6 0.0 reduce-scatter.7.cloned.1.call-start
  39.6 0.7 reduce-scatter.7.cloned.1.call-update
  40.3 0.0 reduce-scatter.11.cloned.1.call-start
  40.4 21.7 %reduce-scatter.9.cloned.1.call-done = bf16[16,1024]{1,0:T(8,128)(2,1)} async-done(((bf16[16,4096]{1,0:T(8,128)(2,1)}), bf16[16,1024]{1,0:T(8,128)(2,1)}) %reduce-scatter.9.cloned.1.call-update) | async-done | bytes 32784 | tf_op jit(solution)/shard_map/reduce_scatter | solution.py:47
  62.1 1.7 convolution_convert_fusion.1
  63.7 0.0 reduce-scatter.11.cloned.1.call-update
  63.8 0.0 all-reduce.3.cloned.1.call-start
  63.8 23.8 %reduce-scatter.7.cloned.1.call-done = bf16[80,1024]{1,0:T(8,128)(2,1)} async-done(((bf16[80,4096]{1,0:T(8,128)(2,1)}), bf16[80,1024]{1,0:T(8,128)(2,1)}) %reduce-scatter.7.cloned.1.call-update) | async-done | bytes 163856 | tf_op jit(solution)/shard_map/reduce_scatter | solution.py:50
  87.6 0.0 all-reduce.3.cloned.1.call-update
  87.6 0.2 reduce-scatter.5.cloned.1.call-start
  87.9 18.3 %fusion.9 = bf16[4096,1024]{1,0:T(8,128)(2,1)} fusion(bf16[1280,4096]{1,0:T(8,128)(2,1)} %param.4, f32[1280,1024]{1,0:T(8,128)} %param.5), kind=kOutput, calls=%fused_computation.12 | convolution fusion | flops 10774380544 | bytes 24117248 | tf_op jit(solution)/shard_map/dot_general | solution.py:28
  106.1 0.0 reduce-scatter.5.cloned.1.call-update
  106.2 2.9 reduce_sum.66
  109.0 21.5 %psum.37 = bf16[1024]{0:T(1024)(128)(2,1)S(1)} all-reduce(bf16[1024]{0:T(1024)(128)(2,1)S(1)} %reduce_sum.66), channel_id=1, replica_groups=mesh['client'=8,'head'=4] {'client'}, use_global_device_ids=true, to_apply=%region_8.9 | all-reduce | flops 1024 | bytes 4096 | tf_op jit(solution)/shard_map/psum | solution.py:56
  130.5 0.6 fusion.18
  131.1 22.5 %reduce-scatter.11.cloned.1.call-done = bf16[16,1024]{1,0:T(8,128)(2,1)} async-done(((bf16[128,1024]{1,0:T(8,128)(2,1)}), bf16[16,1024]{1,0:T(8,128)(2,1)}) %reduce-scatter.11.cloned.1.call-update) | async-done | bytes 32784 | tf_op jit(solution)/shard_map/reduce_scatter | solution.py:60
  153.6 1.4 fusion.16
  155.0 70.9 %all-reduce.3.cloned.1.call-done = bf16[80,1024]{1,0:T(8,128)(2,1)} async-done(((bf16[80,1024]{1,0:T(8,128)(2,1)}), bf16[80,1024]{1,0:T(8,128)(2,1)}) %all-reduce.3.cloned.1.call-update) | async-done | bytes 163856 | tf_op jit(solution)/shard_map/psum | solution.py:55
  225.9 1.6 fusion.15
  228.8 147.9 %reduce-scatter.5.cloned.1.call-done = bf16[512,1024]{1,0:T(8,128)(2,1)} async-done(((bf16[4096,1024]{1,0:T(8,128)(2,1)}), bf16[512,1024]{1,0:T(8,128)(2,1)}) %reduce-scatter.5.cloned.1.call-update) | async-done | bytes 1048592 | tf_op jit(solution)/shard_map/reduce_scatter | solution.py:27
  376.7 2.4 fusion.12
  379.0 39.5 %all-reduce = (f32[]{:T(128)}, f32[]{:T(128)}, f32[]{:T(128)}) all-reduce(f32[]{:T(128)} %fusion.12, f32[]{:T(128)S(6)} %mul.61, f32[]{:T(128)} %fusion.16), channel_id=1, replica_groups=mesh['client'=8,'head'=4] {'client','head'}, use_global_device_ids=true, to_apply=%region_2.3 | all-reduce | flops 3 | bytes 24 | tf_op jit(solution)/shard_map/psum | solution.py:36
  419.9 0.6 convert_multiply_fusion.8
  421.2 1.7 convert_multiply_fusion.4
  422.9 1.4 convert_multiply_fusion.6
  424.3 2.8 convert_multiply_fusion.2
  (3 shorter events, 0.0 us)
Async XLA Ops:
  7.2 54.9 %reduce-scatter.9.cloned.1.call-start = ((), (), s32[]{:S(2)}) async-start(), calls=%async_computation.7 | async-start | bytes 163840 | tf_op jit(solution)/shard_map/reduce_scatter | solution.py:47
  7.2 17.6 %copy-start = (bf16[1280,4096]{1,0:T(8,128)(2,1)S(1)}, bf16[1280,4096]{1,0:T(8,128)(2,1)}, u32[]{:S(2)}) copy-start(bf16[1280,4096]{1,0:T(8,128)(2,1)} %param.4) | copy-start | bytes 31457284
  34.4 27.7 %copy-start.1 = (s32[16]{0:T(128)S(1)}, s32[16]{0:T(128)}, u32[]{:S(2)}) copy-start(s32[16]{0:T(128)} %param.7) | copy-start | bytes 196
  39.6 48.0 %reduce-scatter.7.cloned.1.call-start = ((), (), s32[]{:S(2)}) async-start(), calls=%async_computation.5 | async-start | bytes 819200 | tf_op jit(solution)/shard_map/reduce_scatter | solution.py:50
  40.3 113.3 %reduce-scatter.11.cloned.1.call-start = ((), (), s32[]{:S(2)}) async-start(), calls=%async_computation.8 | async-start | bytes 294912 | tf_op jit(solution)/shard_map/reduce_scatter | solution.py:60
  63.8 162.1 %all-reduce.3.cloned.1.call-start = ((), (), s32[]{:S(2)}) async-start(), calls=%async_computation.6 | async-start | bytes 327680 | tf_op jit(solution)/shard_map/psum | solution.py:55
  87.6 289.0 %reduce-scatter.5.cloned.1.call-start = ((), (), s32[]{:S(2)}) async-start(), calls=%async_computation.4 | async-start | bytes 9437184 | tf_op jit(solution)/shard_map/reduce_scatter | solution.py:27
Sparse Core Ops, SparseCore 0:
  39.7 22.3 reduce-scatter.8
  65.1 22.4 reduce-scatter.6
  91.5 62.0 reduce-scatter.10
  156.8 69.0 all-reduce.2
  229.3 147.2 reduce-scatter.4
where the time goes:
time: 434 us
  waiting for transfers between devices  288 us (66%)
  blocking collectives  61 us (14%)
  matrix products  37.5 us (9%)
  other arithmetic  30 us (7%)
  between operations  17.2 us (4%)
    reduce_scatter x1, waiting for transfers between devices, per_device(): lax.psum_scatter(lax.dot_general(hidden, delta_low, (((0,), (0,)), ((), (...  148 us
    psum x1, waiting for transfers between devices, per_device(): lax.psum(span_part.astype(jnp.bfloat16), 'client').astype(jnp.float32)  70.9 us
    psum x1, blocking collectives, per_device(): head_square = lax.psum(head_square, ('client', 'head'))  39.5 us
    reduce_scatter x1, waiting for transfers between devices, per_device(): lax.psum_scatter(span_whole.astype(jnp.bfloat16), 'head', scatter_dimensi...  23.8 us
    reduce_scatter x1, waiting for transfers between devices, per_device(): lax.psum_scatter(jnp.dot(selector, client_part, precision=lax.Precision.H...  22.5 us
    reduce_scatter x1, waiting for transfers between devices, per_device(): lax.psum_scatter(client_whole.astype(jnp.bfloat16), 'head', scatter_dimen...  21.7 us
    psum x1, blocking collectives, per_device(): lax.psum(bias_local.astype(jnp.bfloat16), 'client').astype(jnp.float32)  21.5 us
    dot_general x1, matrix products, per_device(): lax.dot_general(hidden, delta_low, (((0,), (0,)), ((), ())), preferred_el...  18.3 us
  transfers between devices with their start and end apart: 5, of which 5 were waited for; matrix products, arithmetic and copies ran while one was open for 6% of the time, Pallas kernels for 0%

commit v1 on v0

--- a/solution.py
+++ b/solution.py
@@ -52,7 +52,9 @@
         ).astype(jnp.float32),
     )
     span_raw, bias_raw = (
-        lax.psum(span_part.astype(jnp.bfloat16), "client").astype(jnp.float32),
+        jnp.sum(lax.all_gather(span_part.astype(jnp.bfloat16), "client"), axis=0).astype(
+            jnp.float32
+        ),
         lax.psum(bias_local.astype(jnp.bfloat16), "client").astype(jnp.float32),
     )
     targets = lax.iota(jnp.int32, lax.axis_size("client") * clients_here)

time: 434 us -> 403 us (0.929)
  waiting for transfers between devices: 288 us -> 257 us
    psum x1 -> x0, waiting for transfers between devices: 70.9 us -> none  [per_device(): lax.psum(span_part.astype(jnp.bfloat16), 'client').astype(jnp.float32)]
    all_gather x0 -> x1, waiting for transfers between devices: none -> 41.5 us  [per_device(): lax.all_gather(span_part.astype(jnp.bfloat16), 'client')]
  transfers between devices with their start and end apart: 5 -> 5, of which waited for: 5 -> 5; matrix products, arithmetic and copies ran while one was open for 6% -> 7% of each run, Pallas kernels for 0% -> 0%
where the time goes in v1:
time: 403 us; the launch traced here: 402 us
  waiting for transfers between devices  257 us (64%)
  blocking collectives  61 us (15%)
  matrix products  37.5 us (9%)
  other arithmetic  29.8 us (7%)
  between operations  17.2 us (4%)
    reduce_scatter x1, waiting for transfers between devices, per_device(): lax.psum_scatter(lax.dot_general(hidden, delta_low, (((0,), (0,)), ((), (...  146 us
    all_gather x1, waiting for transfers between devices, per_device(): lax.all_gather(span_part.astype(jnp.bfloat16), 'client')  41.5 us
    psum x1, blocking collectives, per_device(): head_square = lax.psum(head_square, ('client', 'head'))  39.6 us
    reduce_scatter x1, waiting for transfers between devices, per_device(): lax.psum_scatter(span_whole.astype(jnp.bfloat16), 'head', scatter_dimensi...  23.8 us
    reduce_scatter x1, waiting for transfers between devices, per_device(): lax.psum_scatter(jnp.dot(selector, client_part, precision=lax.Precision.H...  22.6 us
    reduce_scatter x1, waiting for transfers between devices, per_device(): lax.psum_scatter(client_whole.astype(jnp.bfloat16), 'head', scatter_dimen...  21.7 us
    psum x1, blocking collectives, per_device(): lax.psum(bias_local.astype(jnp.bfloat16), 'client').astype(jnp.float32)  21.4 us
    dot_general x1, matrix products, per_device(): lax.dot_general(hidden, delta_low, (((0,), (0,)), ((), ())), preferred_el...  18.3 us
  transfers between devices with their start and end apart: 5, of which 5 were waited for; matrix products, arithmetic and copies ran while one was open for 7% of the time, Pallas kernels for 0%

profile of v1, /device:TPU:0, one launch (start us, length us, event | category | flops | bytes accessed | tf_op | source)
XLA Modules:
  0.0 402.5 jit_solution(3674433585175292580)
XLA Ops:
  7.2 0.0 reduce-scatter.9.cloned.1.call-start
  7.2 17.6 %convolution_convert_fusion = bf16[1280,4096]{1,0:T(8,128)(2,1)} fusion(bf16[4096,1024]{1,0:T(8,128)(2,1)} %param.6, f32[1280,1024]{1,0:T(8,128)} %param.5), kind=kOutput, calls=%fused_computation.10 | convolution fusion | flops 10743971840 | bytes 24117248 | tf_op jit(solution)/shard_map/dot_general | solution.py:38
  24.8 9.6 %fusion.6 = f32[1280,4096]{1,0:T(8,128)S(1)} fusion(bf16[1280,4096]{1,0:T(8,128)(2,1)S(1)} %copy-done, bf16[1280,4096]{1,0:T(8,128)(2,1)} %convolution_convert_fusion), kind=kLoop, calls=%fused_computation.9 | loop fusion | flops 52428800 | bytes 41943040 | tf_op jit(solution)/shard_map/mul | solution.py:42
  34.4 5.2 %fusion.20 = (bf16[16,4096]{1,0:T(8,128)(2,1)}, bf16[80,4096]{1,0:T(8,128)(2,1)}) fusion(f32[16,80,4096]{2,1,0:T(8,128)S(1)} %bitcast.4), kind=kLoop, calls=%fused_computation.31 | loop fusion | flops 10092544 | bytes 21757952 | tf_op jit(solution)/shard_map/reduce_sum | solution.py:44
  39.5 0.0 reduce-scatter.9.cloned.1.call-update
  39.6 0.0 reduce-scatter.7.cloned.1.call-start
  39.6 0.7 reduce-scatter.7.cloned.1.call-update
  40.3 0.0 reduce-scatter.11.cloned.1.call-start
  40.4 21.7 %reduce-scatter.9.cloned.1.call-done = bf16[16,1024]{1,0:T(8,128)(2,1)} async-done(((bf16[16,4096]{1,0:T(8,128)(2,1)}), bf16[16,1024]{1,0:T(8,128)(2,1)}) %reduce-scatter.9.cloned.1.call-update) | async-done | bytes 32784 | tf_op jit(solution)/shard_map/reduce_scatter | solution.py:47
  62.1 1.7 convolution_convert_fusion.1
  63.7 0.0 reduce-scatter.11.cloned.1.call-update
  63.8 0.0 all-gather.3.cloned.1.call-start
  63.8 23.8 %reduce-scatter.7.cloned.1.call-done = bf16[80,1024]{1,0:T(8,128)(2,1)} async-done(((bf16[80,4096]{1,0:T(8,128)(2,1)}), bf16[80,1024]{1,0:T(8,128)(2,1)}) %reduce-scatter.7.cloned.1.call-update) | async-done | bytes 163856 | tf_op jit(solution)/shard_map/reduce_scatter | solution.py:50
  87.6 0.0 all-gather.3.cloned.1.call-update
  87.6 0.2 reduce-scatter.5.cloned.1.call-start
  87.9 18.3 %fusion.9 = bf16[4096,1024]{1,0:T(8,128)(2,1)} fusion(bf16[1280,4096]{1,0:T(8,128)(2,1)} %param.4, f32[1280,1024]{1,0:T(8,128)} %param.5), kind=kOutput, calls=%fused_computation.12 | convolution fusion | flops 10774380544 | bytes 24117248 | tf_op jit(solution)/shard_map/dot_general | solution.py:28
  106.1 0.0 reduce-scatter.5.cloned.1.call-update
  106.2 2.9 reduce_sum.79
  109.0 21.4 %psum.29 = bf16[1024]{0:T(1024)(128)(2,1)S(1)} all-reduce(bf16[1024]{0:T(1024)(128)(2,1)S(1)} %reduce_sum.79), channel_id=1, replica_groups=mesh['client'=8,'head'=4] {'client'}, use_global_device_ids=true, to_apply=%region_8.9 | all-reduce | flops 1024 | bytes 4096 | tf_op jit(solution)/shard_map/psum | solution.py:58
  130.5 0.6 fusion.18
  131.1 22.6 %reduce-scatter.11.cloned.1.call-done = bf16[16,1024]{1,0:T(8,128)(2,1)} async-done(((bf16[128,1024]{1,0:T(8,128)(2,1)}), bf16[16,1024]{1,0:T(8,128)(2,1)}) %reduce-scatter.11.cloned.1.call-update) | async-done | bytes 32784 | tf_op jit(solution)/shard_map/reduce_scatter | solution.py:62
  153.6 1.4 fusion.16
  155.0 41.5 %all-gather.3.cloned.1.call-done = bf16[640,1024]{1,0:T(8,128)(2,1)} async-done(((bf16[80,1024]{1,0:T(8,128)(2,1)}), bf16[640,1024]{1,0:T(8,128)(2,1)}) %all-gather.3.cloned.1.call-update) | async-done | bytes 1310736 | tf_op jit(solution)/shard_map/all_gather | solution.py:55
  196.6 1.6 reduce_sum.77
  198.1 0.7 fusion.15
  200.1 146.3 %reduce-scatter.5.cloned.1.call-done = bf16[512,1024]{1,0:T(8,128)(2,1)} async-done(((bf16[4096,1024]{1,0:T(8,128)(2,1)}), bf16[512,1024]{1,0:T(8,128)(2,1)}) %reduce-scatter.5.cloned.1.call-update) | async-done | bytes 1048592 | tf_op jit(solution)/shard_map/reduce_scatter | solution.py:27
  346.4 2.4 fusion.12
  348.8 39.6 %all-reduce = (f32[]{:T(128)}, f32[]{:T(128)}, f32[]{:T(128)}) all-reduce(f32[]{:T(128)} %fusion.12, f32[]{:T(128)S(6)} %mul.61, f32[]{:T(128)} %fusion.16), channel_id=1, replica_groups=mesh['client'=8,'head'=4] {'client','head'}, use_global_device_ids=true, to_apply=%region_2.3 | all-reduce | flops 3 | bytes 24 | tf_op jit(solution)/shard_map/psum | solution.py:36
  389.0 0.8 convert_multiply_fusion.4
  389.8 0.6 convert_multiply_fusion.8
  391.7 1.4 convert_multiply_fusion.6
  393.1 2.8 convert_multiply_fusion.2
  (4 shorter events, 0.0 us)
Async XLA Ops:
  7.2 54.9 %reduce-scatter.9.cloned.1.call-start = ((), (), s32[]{:S(2)}) async-start(), calls=%async_computation.6 | async-start | bytes 163840 | tf_op jit(solution)/shard_map/reduce_scatter | solution.py:47
  7.2 17.6 %copy-start = (bf16[1280,4096]{1,0:T(8,128)(2,1)S(1)}, bf16[1280,4096]{1,0:T(8,128)(2,1)}, u32[]{:S(2)}) copy-start(bf16[1280,4096]{1,0:T(8,128)(2,1)} %param.4) | copy-start | bytes 31457284
  34.4 27.7 %copy-start.1 = (s32[16]{0:T(128)S(1)}, s32[16]{0:T(128)}, u32[]{:S(2)}) copy-start(s32[16]{0:T(128)} %param.7) | copy-start | bytes 196
  39.6 48.0 %reduce-scatter.7.cloned.1.call-start = ((), (), s32[]{:S(2)}) async-start(), calls=%async_computation.5 | async-start | bytes 819200 | tf_op jit(solution)/shard_map/reduce_scatter | solution.py:50
  40.3 113.3 %reduce-scatter.11.cloned.1.call-start = ((), (), s32[]{:S(2)}) async-start(), calls=%async_computation.7 | async-start | bytes 294912 | tf_op jit(solution)/shard_map/reduce_scatter | solution.py:62
  63.8 132.8 %all-gather.3.cloned.1.call-start = ((), (), s32[]{:S(2)}) async-start(), calls=%async_computation.8 | async-start | bytes 1474560 | tf_op jit(solution)/shard_map/all_gather | solution.py:55
  87.6 258.7 %reduce-scatter.5.cloned.1.call-start = ((), (), s32[]{:S(2)}) async-start(), calls=%async_computation.4 | async-start | bytes 9437184 | tf_op jit(solution)/shard_map/reduce_scatter | solution.py:27
Sparse Core Ops, SparseCore 0:
  39.7 22.3 reduce-scatter.8
  65.1 22.4 reduce-scatter.6
  91.5 62.0 reduce-scatter.10
  155.7 40.8 all-gather.2
  200.0 146.3 reduce-scatter.4
